TPU v7x, 32 devices: a whole 2x2x4 slice. The times are simulated.
32 devices in a mesh: ex: 4 (over z), tp: 4 (over y, x), dp: 2 (over core).
Axes of the slice: x: 2, y: 2, z: 4, core: 2. Of those that a mesh axis runs over, the one named last changes fastest.
Arguments:
- tokens: bfloat16 [1024, 2880], P(('ex', 'dp')), may hold values from -32 to 32
- route_one: int32 [1024, 4], P(('ex', 'dp')), may hold values from 0 to 15, as said below
- route_two: int32 [1024, 4], P(('ex', 'dp')), may hold values from 0 to 15, as said below
- share_one: float32 [1024, 4], P(('ex', 'dp')), may hold values from 0.05 to 0.6
- share_two: float32 [1024, 4], P(('ex', 'dp')), may hold values from 0.05 to 0.6
- gain_one: float32 [2880], replicated, may hold values from 0.5 to 1.5
- gain_two: float32 [2880], replicated, may hold values from 0.5 to 1.5
- gate_up_one: bfloat16 [16, 2880, 2, 2880], P('ex', None, None, 'tp'), may hold values from -0.109375 to 0.109375
- down_one: bfloat16 [16, 2880, 2880], P('ex', 'tp'), may hold values from -0.109375 to 0.109375
- gate_up_two: bfloat16 [16, 2880, 2, 2880], P('ex', None, None, 'tp'), may hold values from -0.109375 to 0.109375
- down_two: bfloat16 [16, 2880, 2880], P('ex', 'tp'), may hold values from -0.109375 to 0.109375
Outputs:
- mixed: bfloat16 [1024, 2880], P(('ex', 'dp'), 'tp')
- load: int32 [2, 16], P(None, 'ex')
Inputs may be any that keep to these rules, and one draw needn't show every extreme that they name: `route_one`: each row names 4 different experts; in each aligned block of 128 rows no expert is named by more than 64 rows, and in every block some expert is named by exactly 64 rows. `route_two`: each row names 4 different experts; in each aligned block of 128 rows no expert is named by more than 64 rows, and in every block some expert is named by exactly 64 rows.
All inputs are finite; a program needn't handle non-finite values.
Results may differ from a plain program's by a relative error of at most 0.011.
Values may be sent and summed in bfloat16 or wider, within the bound.
A program may use at most 192 MiB of HBM per device.

v0:
```python
import jax
import jax.numpy as jnp
from jax import lax
from jax.sharding import PartitionSpec as P

norm_eps = 1e-05
glu_alpha = 1.702


def normalize(stream, gains):
    values = stream.astype(jnp.float32)
    inverse = lax.rsqrt(jnp.mean(values * values, axis=1, keepdims=True) + norm_eps)
    return (values * inverse * gains[None, :]).astype(jnp.bfloat16)


def placement(routes, experts, capacity):
    tokens_here = routes.shape[0]
    top_count = routes.shape[1]
    flattened = routes.reshape(tokens_here * top_count)
    matches = (flattened[:, None] == jnp.arange(experts, dtype=jnp.int32)[None, :]).astype(
        jnp.int32
    )
    slot_rank = jnp.cumsum(matches, axis=0) - 1
    slot_index = jnp.sum(slot_rank * matches, axis=1)
    target = (flattened * capacity + slot_index).reshape(tokens_here, top_count)
    return (target, jnp.sum(matches, axis=0))


def pack_rows(target, normed, total_slots):
    wanted = jnp.arange(total_slots, dtype=jnp.int32)[:, None, None] == target[None, :, :]
    chooser = jnp.any(wanted, axis=2).astype(jnp.bfloat16)
    return jnp.dot(chooser, normed, preferred_element_type=jnp.float32).astype(jnp.bfloat16)


def activate(hidden, share_width):
    gate_part = hidden[..., :share_width]
    up_part = hidden[..., share_width:]
    return (gate_part * jax.nn.sigmoid(glu_alpha * gate_part) * (up_part + 1.0)).astype(
        jnp.bfloat16
    )


def expert_layer(stream, routes, shares, gains, gate_up, down_proj):
    ex_count = lax.axis_size("ex")
    tp_count = lax.axis_size("tp")
    tp_place = lax.axis_index("tp")
    local_count = gate_up.shape[0]
    model_width = gate_up.shape[1]
    share_width = gate_up.shape[3]
    experts = local_count * ex_count
    tokens_here = routes.shape[0]
    top_count = routes.shape[1]
    capacity = 2 * tokens_here * top_count // experts
    col_share = model_width // tp_count
    normed = normalize(stream, gains)
    target, counted = placement(routes, experts, capacity)
    gate_up_flat = gate_up.reshape(local_count, model_width, 2 * share_width)
    counts_out = counted.reshape(ex_count, local_count)
    packed = pack_rows(target, normed, experts * capacity).reshape(
        ex_count, local_count, capacity, model_width
    )
    arrived, arrived_counts = (
        lax.all_to_all(packed, "ex", split_axis=0, concat_axis=0, tiled=True),
        lax.all_to_all(counts_out, "ex", split_axis=0, concat_axis=0, tiled=True),
    )
    hidden = jnp.einsum("secd,edf->secf", arrived, gate_up_flat, preferred_element_type=jnp.float32)
    activated = activate(hidden, share_width)
    partial_value = jnp.einsum(
        "secf,efd->secd", activated, down_proj, preferred_element_type=jnp.float32
    )
    partial_value = lax.optimization_barrier(partial_value.astype(jnp.bfloat16)).astype(jnp.float32)
    resident = stream.astype(jnp.float32)
    expert_rows = lax.psum_scatter(
        partial_value.astype(jnp.bfloat16), "tp", scatter_dimension=3, tiled=True
    )
    returned = lax.all_to_all(expert_rows, "ex", split_axis=0, concat_axis=0, tiled=True)
    residual = lax.dynamic_slice_in_dim(resident, tp_place * col_share, col_share, 1)
    out_width = returned.shape[3]
    flat_returned = returned.reshape(experts * capacity, out_width)
    picked = jnp.take(flat_returned, target.reshape(tokens_here * top_count), axis=0)
    picked = picked.reshape(tokens_here, top_count, out_width).astype(jnp.float32)
    mixed = residual + jnp.sum(shares[:, :, None] * picked, axis=1)
    return (mixed.astype(jnp.bfloat16), jnp.sum(arrived_counts, axis=0))


def body(
    tokens,
    route_one,
    route_two,
    share_one,
    share_two,
    gain_one,
    gain_two,
    gate_up_one,
    down_one,
    gate_up_two,
    down_two,
):
    first_out, load_first = expert_layer(
        tokens, route_one, share_one, gain_one, gate_up_one, down_one
    )
    stream = lax.all_gather(first_out, "tp", axis=1, tiled=True)
    second, load_second = expert_layer(
        stream, route_two, share_two, gain_two, gate_up_two, down_two
    )
    load_pair = lax.psum(jnp.stack([load_first, load_second]), "dp").astype(jnp.int32)
    return (second, load_pair)


def solution(mesh):
    in_specs = (
        P(("ex", "dp"), None),
        P(("ex", "dp"), None),
        P(("ex", "dp"), None),
        P(("ex", "dp"), None),
        P(("ex", "dp"), None),
        P(),
        P(),
        P("ex", None, None, "tp"),
        P("ex", "tp", None),
        P("ex", None, None, "tp"),
        P("ex", "tp", None),
    )
    out_specs = (P(("ex", "dp"), "tp"), P(None, "ex"))
    return jax.shard_map(body, mesh=mesh, in_specs=in_specs, out_specs=out_specs, check_vma=False)
```

profile of v0, /device:TPU:0, one launch (start us, length us, event | category | flops | bytes accessed | tf_op | source)
XLA Modules:
  0.0 731.7 jit_solution(12624737005077920805)
XLA Ops:
  7.2 0.8 copy.111
  8.2 1.2 reduce-window.14
  10.0 0.7 multiply_add_fusion.1
  10.7 0.4 fusion.22
  11.0 1.5 copy.109
  12.7 5.1 convolution_convert_fusion.1
  17.8 8.5 %copy.115 = bf16[1024,2880]{1,0:T(8,128)(2,1)} copy(bf16[1024,2880]{0,1:T(8,128)(2,1)} %convolution_convert_fusion.1) | data formatting | bytes 11796480 | tf_op jit(solution)/shard_map/convert_element_type | solution.py:32
  26.3 141.0 %all_to_all.38 = bf16[4,4,64,2880]{3,2,1,0:T(8,128)(2,1)} all-to-all(bf16[4,4,64,2880]{3,2,1,0:T(8,128)(2,1)} %bitcast.86), channel_id=1, replica_groups=mesh['ex'=4,'tp'=4,'dp'=2] {'ex'}, dimensions={0} | all-to-all | bytes 11796480 | tf_op jit(solution)/shard_map/all_to_all | solution.py:63
  167.4 19.2 %fusion.12 = f32[4,4,64,1440]{3,2,0,1:T(8,128)} fusion(bf16[4,2880,1440,1]{1,2,3,0:T(8,128)(2,1)} %bitcast.82, bf16[4,4,64,2880]{3,2,1,0:T(8,128)(2,1)} %all_to_all.38), kind=kOutput, calls=%fused_computation.14 | convolution fusion | flops 8493465600 | bytes 44974080 | tf_op jit(solution)/shard_map/secd,edf->secf/dot_general | solution.py:66
  186.5 14.2 %convert_bitcast_fusion.1 = bf16[4,4,64,2880]{3,2,0,1:T(8,128)(2,1)} fusion(bf16[4,720,2880]{2,1,0:T(8,128)(2,1)} %param.21, f32[4,4,64,1440]{3,2,0,1:T(8,128)} %fusion.12), kind=kOutput, calls=%fused_computation.11 | convolution fusion | flops 4255580160 | bytes 28385280 | tf_op jit(solution)/shard_map/secf,efd->secd/dot_general | solution.py:68
  200.7 19.2 %copy.135 = bf16[4,4,64,2880]{2,0,1,3:T(4,128)(2,1)} copy(bf16[4,4,64,2880]{3,2,0,1:T(8,128)(2,1)} %convert_bitcast_fusion.1) | data formatting | bytes 11796480
  219.9 19.0 %reshape.149 = bf16[2880,1024]{1,0:T(8,128)(2,1)} reshape(bf16[2880,4,4,64]{3,2,1,0:T(4,128)(2,1)} %bitcast.80) | data formatting | bytes 11796480
  239.0 65.9 %reduce-scatter.7.cloned.1.call-done = bf16[720,1024]{1,0:T(8,128)(2,1)} async-done(((bf16[2880,1024]{1,0:T(8,128)(2,1)}), bf16[720,1024]{1,0:T(8,128)(2,1)}) %reduce-scatter.7.cloned.1.call-update) | async-done | bytes 1474576
  304.9 6.4 reshape.150
  311.3 5.6 copy.117
  316.9 4.7 all-to-all-start.1
  321.6 1.3 convert_element_type.76
  323.3 1.2 reduce-window.16
  325.1 0.4 fusion.23
  325.5 32.9 %all-to-all-done.1 = bf16[4,4,64,720]{3,2,1,0:T(8,128)(2,1)S(1)} async-done(((bf16[4,4,64,720]{3,2,1,0:T(8,128)(2,1)}), bf16[4,4,64,720]{3,2,1,0:T(8,128)(2,1)S(1)}, u32[]{:S(2)}, u32[]{:S(2)}) %all-to-all-start.1) | async-done | bytes 1474592 | tf_op jit(solution)/shard_map/all_to_all | solution.py:76
  358.4 2.0 gather_fusion
  360.6 0.5 reshape.121
  361.1 1.0 multiply_reduce_fusion.1
  362.1 1.2 add_convert_fusion.1
  363.5 11.6 %all_gather.3 = bf16[128,2880]{0,1:T(8,128)(2,1)S(1)} all-gather(bf16[128,720]{0,1:T(8,128)(2,1)S(1)} %copy.118), channel_id=1, replica_groups=mesh['ex'=4,'tp'=4,'dp'=2] {'tp'}, dimensions={1}, use_global_device_ids=true | all-gather | bytes 921600 | tf_op jit(solution)/shard_map/all_gather | solution.py:102
  375.6 4.4 convolution_convert_fusion
  380.0 8.5 %copy.125 = bf16[1024,2880]{1,0:T(8,128)(2,1)} copy(bf16[1024,2880]{0,1:T(8,128)(2,1)} %convolution_convert_fusion) | data formatting | bytes 11796480 | tf_op jit(solution)/shard_map/convert_element_type | solution.py:32
  388.5 136.0 %all_to_all.39 = bf16[4,4,64,2880]{3,2,1,0:T(8,128)(2,1)} all-to-all(bf16[4,4,64,2880]{3,2,1,0:T(8,128)(2,1)} %bitcast.87), channel_id=1, replica_groups=mesh['ex'=4,'tp'=4,'dp'=2] {'ex'}, dimensions={0} | all-to-all | bytes 11796480 | tf_op jit(solution)/shard_map/all_to_all | solution.py:63
  524.5 19.2 %fusion.15 = f32[4,4,64,1440]{3,2,0,1:T(8,128)} fusion(bf16[4,2880,1440,1]{1,2,3,0:T(8,128)(2,1)} %bitcast.83, bf16[4,4,64,2880]{3,2,1,0:T(8,128)(2,1)} %all_to_all.39), kind=kOutput, calls=%fused_computation.15 | convolution fusion | flops 8493465600 | bytes 44974080 | tf_op jit(solution)/shard_map/secd,edf->secf/dot_general | solution.py:66
  543.7 14.2 %convert_bitcast_fusion = bf16[4,4,64,2880]{3,2,0,1:T(8,128)(2,1)} fusion(bf16[4,720,2880]{2,1,0:T(8,128)(2,1)} %param.23, f32[4,4,64,1440]{3,2,0,1:T(8,128)} %fusion.15), kind=kOutput, calls=%fused_computation.10 | convolution fusion | flops 4255580160 | bytes 28385280 | tf_op jit(solution)/shard_map/secf,efd->secd/dot_general | solution.py:68
  558.0 19.2 %copy.137 = bf16[4,4,64,2880]{2,0,1,3:T(4,128)(2,1)} copy(bf16[4,4,64,2880]{3,2,0,1:T(8,128)(2,1)} %convert_bitcast_fusion) | data formatting | bytes 11796480
  577.1 19.0 %reshape.151 = bf16[2880,1024]{1,0:T(8,128)(2,1)} reshape(bf16[2880,4,4,64]{3,2,1,0:T(4,128)(2,1)} %bitcast.81) | data formatting | bytes 11796480
  596.2 0.7 all_to_all.28
  596.9 3.2 all-to-all-start.4
  600.1 0.7 all_to_all.30
  600.8 60.5 %reduce-scatter.9.cloned.1.call-done = bf16[720,1024]{1,0:T(8,128)(2,1)} async-done(((bf16[2880,1024]{1,0:T(8,128)(2,1)}), bf16[720,1024]{1,0:T(8,128)(2,1)}) %reduce-scatter.9.cloned.1.call-update) | async-done | bytes 1474576
  661.2 6.4 reshape.152
  667.7 4.6 all-to-all-start.5
  672.2 5.6 copy.127
  677.8 5.1 all-to-all-start.3
  683.1 2.4 psum.7
  685.5 1.3 convert_element_type.86
  686.8 32.4 %all-to-all-done.3 = bf16[4,4,64,720]{3,2,1,0:T(8,128)(2,1)S(1)} async-done(((bf16[4,4,64,720]{3,2,1,0:T(8,128)(2,1)}), bf16[4,4,64,720]{3,2,1,0:T(8,128)(2,1)S(1)}, u32[]{:S(2)}, u32[]{:S(2)}) %all-to-all-start.3) | async-done | bytes 1474592 | tf_op jit(solution)/shard_map/all_to_all | solution.py:76
  719.2 2.0 gather_fusion.1
  721.4 0.5 reshape.122
  721.8 1.0 multiply_reduce_fusion
  722.9 1.2 add_convert_fusion
  724.1 0.8 copy.130
  (51 shorter events, 3.5 us)
Async XLA Ops:
  7.2 297.7 %reduce-scatter.7.cloned.1.call-start = ((), (), s32[]{:S(2)}) async-start(), calls=%async_computation.8 | async-start | bytes 7372800
  316.9 6.0 copy-start.1
  316.9 6.3 copy-start.2
  316.9 41.5 %all-to-all-start.1 = ((bf16[4,4,64,720]{3,2,1,0:T(8,128)(2,1)}), bf16[4,4,64,720]{3,2,1,0:T(8,128)(2,1)S(1)}, u32[]{:S(2)}, u32[]{:S(2)}) async-start(bf16[4,4,64,720]{3,2,1,0:T(8,128)(2,1)} %copy.117), calls=%async_computation.1 | async-start | bytes 3145728 | tf_op jit(solution)/shard_map/all_to_all | solution.py:76
  321.6 339.6 %reduce-scatter.9.cloned.1.call-start = ((), (), s32[]{:S(2)}) async-start(), calls=%async_computation.9 | async-start | bytes 7372800
  361.1 14.6 %copy-start = (f32[2880]{0:T(1024)S(1)}, f32[2880]{0:T(1024)}, u32[]{:S(2)}) copy-start(f32[2880]{0:T(1024)} %param.19) | copy-start | bytes 34564
  596.9 70.8 %all-to-all-start.4 = ((s32[4,1,4]{2,1,0:T(1,128)}), s32[4,1,4]{2,1,0:T(1,128)S(1)}, u32[]{:S(2)}, u32[]{:S(2)}) async-start(s32[4,1,4]{2,1,0:T(1,128)} %bitcast.20), calls=%async_computation.4 | async-start | bytes 4096 | tf_op jit(solution)/shard_map/all_to_all | solution.py:64
  667.7 10.2 %all-to-all-start.5 = ((s32[4,1,4]{2,1,0:T(1,128)}), s32[4,1,4]{2,1,0:T(1,128)S(1)}, u32[]{:S(2)}, u32[]{:S(2)}) async-start(s32[4,1,4]{2,1,0:T(1,128)} %bitcast.22), calls=%async_computation.5 | async-start | bytes 4096 | tf_op jit(solution)/shard_map/all_to_all | solution.py:64
  672.2 10.8 %copy-start.3 = (f32[128,4]{0,1:T(4,128)S(1)}, f32[128,4]{0,1:T(4,128)}, u32[]{:S(2)}) copy-start(f32[128,4]{0,1:T(4,128)} %param.17) | copy-start | bytes 6148
  677.8 41.3 %all-to-all-start.3 = ((bf16[4,4,64,720]{3,2,1,0:T(8,128)(2,1)}), bf16[4,4,64,720]{3,2,1,0:T(8,128)(2,1)S(1)}, u32[]{:S(2)}, u32[]{:S(2)}) async-start(bf16[4,4,64,720]{3,2,1,0:T(8,128)(2,1)} %copy.127), calls=%async_computation.3 | async-start | bytes 3145728 | tf_op jit(solution)/shard_map/all_to_all | solution.py:76
Sparse Core Ops, SparseCore 0:
  239.1 65.7 reduce-scatter.6
  596.3 64.8 reduce-scatter.8
where the time goes:
time: 735 us; the launch traced here: 732 us
  blocking collectives  291 us (40%)
  waiting for transfers between devices  192 us (26%)
  local copies, waits for them, and re-layouts  129 us (18%)
  matrix products  76.3 us (10%)
  starting transfers between devices  17.7 us (2%)
  between operations  14.3 us (2%)
  other arithmetic  11.9 us (2%)
    all_to_all x2, blocking collectives, expert_layer(): lax.all_to_all(packed, 'ex', split_axis=0, concat_axis=0, tiled=True)  277 us
    unnamed x4, waiting for transfers between devices  126 us
    unnamed x20, local copies, waits for them, and re-layouts  92.6 us
    all_to_all x2, waiting for transfers between devices, expert_layer(): lax.all_to_all(expert_rows, 'ex', split_axis=0, concat_axis=0, tiled=True)  65.3 us
    dot_general x2, matrix products, expert_layer(): jnp.einsum('secd,edf->secf', arrived, gate_up_flat, preferred_element_typ...  38.3 us
    dot_general x2, matrix products, expert_layer(): jnp.einsum('secf,efd->secd', activated, down_proj, preferred_element_type...  28.5 us
    convert_element_type x2, local copies, waits for them, and re-layouts, pack_rows(): jnp.dot(chooser, normed, preferred_element_type=jnp.float32)  17 us
  transfers between devices with their start and end apart: 6, of which 4 were waited for; matrix products, arithmetic and copies ran while one was open for 2% of the time, Pallas kernels for 0%

commit v1 on v0

v1 whole, which is shorter than its diff:
```python
import functools

import jax
import jax.numpy as jnp
from jax import lax
from jax.experimental import pallas as pl
from jax.experimental.pallas import tpu as pltpu
from jax.sharding import PartitionSpec as P

norm_eps = 1e-05
glu_alpha = 1.702


def placement(routes, experts, capacity):
    tokens_here, top_count = routes.shape
    flattened = routes.reshape(tokens_here * top_count)
    matches = (flattened[:, None] == jnp.arange(experts, dtype=jnp.int32)[None, :]).astype(
        jnp.int32
    )
    slot_rank = jnp.cumsum(matches, axis=0) - 1
    slot_index = jnp.sum(slot_rank * matches, axis=1)
    target = (flattened * capacity + slot_index).reshape(tokens_here, top_count)
    return target


def choosers(target, shares, local_count, capacity, group):
    sources, top_count, tokens_here = target.shape
    groups = sources // group
    wide = group * capacity
    first = lax.axis_index("ex") * (local_count * capacity)
    local = target.astype(jnp.int32) - first
    inside = (local >= 0) & (local < local_count * capacity)
    place = (jnp.arange(sources, dtype=jnp.int32) % group)[:, None, None]
    column = (local // capacity) * wide + place * capacity + local % capacity
    column = jnp.where(inside, column, -1)
    column = column.reshape(groups, group, top_count, tokens_here)
    column = column.transpose(0, 1, 3, 2).reshape(groups, group * tokens_here, top_count)
    share = shares.reshape(groups, group, top_count, tokens_here)
    share = share.transpose(0, 1, 3, 2).reshape(groups, group * tokens_here, top_count)
    slots = jnp.arange(local_count * wide, dtype=jnp.int32)
    equal = column[:, :, :, None] == slots
    chooser = jnp.any(equal, axis=2).astype(jnp.bfloat16)
    weight = jnp.sum(jnp.where(equal, share[:, :, :, None], 0.0), axis=(1, 2))
    weight = weight.reshape(groups, local_count, wide).transpose(1, 0, 2)
    return chooser, weight.reshape(local_count, 1, groups * wide)


def expert_kernel(group, x_ref, gain_ref, choose_ref, weight_ref, up_ref, down_ref, y_ref,
                  packed, outs):
    step = pl.program_id(0)
    steps = pl.num_programs(0)
    sources, width, tokens_here = x_ref.shape
    groups = sources // group
    wide = packed.shape[1] // groups
    share_width = down_ref.shape[1]

    @pl.when(step == 0)
    def _():
        for s in range(sources):
            values = x_ref[s].astype(jnp.float32)
            inverse = lax.rsqrt(jnp.mean(values * values, axis=0, keepdims=True) + norm_eps)
            y_ref[s] = (values * inverse * gain_ref[...]).astype(jnp.bfloat16)

    at = pl.multiple_of(step * wide, wide)
    for g in range(groups):
        normed = [y_ref[g * group + s] for s in range(group)]
        normed = jnp.concatenate(normed, axis=1)
        packed[:, g * wide:(g + 1) * wide] = jnp.dot(
            normed, choose_ref[g, :, pl.ds(at, wide)], preferred_element_type=jnp.float32
        ).astype(jnp.bfloat16)
    gate = jnp.dot(up_ref[0, :share_width], packed[...], preferred_element_type=jnp.float32)
    up = jnp.dot(up_ref[0, share_width:], packed[...], preferred_element_type=jnp.float32)
    act = gate * jax.nn.sigmoid(glu_alpha * gate) * (up + 1.0) * weight_ref[0]
    act = act.T.astype(jnp.bfloat16)
    out = jnp.dot(act, down_ref[0], preferred_element_type=jnp.float32).astype(jnp.bfloat16)
    for g in range(groups):
        outs[g, pl.ds(at, wide)] = out[g * wide:(g + 1) * wide]

    @pl.when(step == steps - 1)
    def _():
        for g in range(groups):
            mixed = jnp.dot(choose_ref[g], outs[g], preferred_element_type=jnp.float32)
            mixed = mixed.astype(jnp.bfloat16).T
            for s in range(group):
                y_ref[g * group + s] = mixed[:, s * tokens_here:(s + 1) * tokens_here]


def experts_here(x, gains, chooser, weight, gate_up, down_proj, group):
    sources, width, tokens_here = x.shape
    local_count, _, share_width = gate_up.shape[0], gate_up.shape[2], gate_up.shape[3]
    groups = sources // group
    slots = weight.shape[2]
    wide = slots // groups
    rows_in = gate_up.transpose(0, 2, 3, 1).reshape(local_count, 2 * share_width, width)
    whole = lambda shape: pl.BlockSpec(shape, lambda e: (0,) * len(shape))
    return pl.pallas_call(
        functools.partial(expert_kernel, group),
        grid=(local_count,),
        out_shape=jax.ShapeDtypeStruct((sources, width, tokens_here), jnp.bfloat16),
        in_specs=[
            whole(x.shape),
            whole((width, 1)),
            whole(chooser.shape),
            pl.BlockSpec((1, 1, slots), lambda e: (e, 0, 0)),
            pl.BlockSpec((1, 2 * share_width, width), lambda e: (e, 0, 0)),
            pl.BlockSpec((1, share_width, width), lambda e: (e, 0, 0)),
        ],
        out_specs=whole(x.shape),
        scratch_shapes=[
            pltpu.VMEM((width, slots), jnp.bfloat16),
            pltpu.VMEM((groups, local_count * wide, width), jnp.bfloat16),
        ],
        compiler_params=pltpu.CompilerParams(
            dimension_semantics=("arbitrary",), vmem_limit_bytes=60 * 1024 * 1024
        ),
        cost_estimate=pl.CostEstimate(
            flops=6 * local_count * slots * width * share_width,
            bytes_accessed=6 * local_count * width * share_width,
            transcendentals=0,
        ),
        name="experts_here",
    )(x, gains[:, None], chooser, weight, rows_in, down_proj)


MESH = pl.DeviceIdType.MESH


def greet(with_dp=False):
    barrier = pltpu.get_barrier_semaphore()
    total = 0
    for axis in ("ex", "tp"):
        count = lax.axis_size(axis)
        for ahead in range(1, count):
            peer = lax.rem(lax.axis_index(axis) + ahead, count)
            pl.semaphore_signal(barrier, inc=1, device_id={axis: peer}, device_id_type=MESH)
            total += 1
    if with_dp:
        for peer in dp_peers():
            pl.semaphore_signal(barrier, inc=1, device_id=peer, device_id_type=MESH)
            total += 1
    pl.semaphore_wait(barrier, total)


def dp_peers():
    ex_count, dp_count = lax.axis_size("ex"), lax.axis_size("dp")
    return [
        {
            "ex": lax.rem(lax.axis_index("ex") + ahead, ex_count),
            "dp": lax.rem(lax.axis_index("dp") + across, dp_count),
        }
        for across in range(1, dp_count)
        for ahead in range(ex_count)
    ]


def gather_small_kernel(own_ref, small_ref, all_ref, smalls_ref, send_ex, recv_ex, send_tp,
                        recv_tp, send_small, recv_small):
    ex, dp = lax.axis_index("ex"), lax.axis_index("dp")
    ex_count = lax.axis_size("ex")
    greet(True)
    peers = [
        {"ex": lax.rem(ex + ahead, ex_count), "dp": dp} for ahead in range(1, ex_count)
    ] + dp_peers()
    copies = []
    for at, peer in enumerate(peers):
        copy = pltpu.make_async_remote_copy(
            src_ref=small_ref,
            dst_ref=smalls_ref.at[dp, ex],
            send_sem=send_small.at[at],
            recv_sem=recv_small.at[at],
            device_id=peer,
            device_id_type=MESH,
        )
        copy.start()
        copies.append(copy)
    smalls_ref[dp, ex] = small_ref[...]
    gather_steps(own_ref, all_ref, send_ex, recv_ex, send_tp, recv_tp)
    for copy in copies:
        copy.wait_recv()
    for copy in copies:
        copy.wait_send()


def gather_kernel(own_ref, all_ref, send_ex, recv_ex, send_tp, recv_tp):
    greet()
    gather_steps(own_ref, all_ref, send_ex, recv_ex, send_tp, recv_tp)


def gather_steps(own_ref, all_ref, send_ex, recv_ex, send_tp, recv_tp):
    ex_count, tp_count = all_ref.shape[:2]
    ex, tp = lax.axis_index("ex"), lax.axis_index("tp")
    started = []

    def push(source, block, axis, index, count, ahead, send, recv):
        copy = pltpu.make_async_remote_copy(
            src_ref=source,
            dst_ref=all_ref.at[block, tp],
            send_sem=send,
            recv_sem=recv,
            device_id={axis: lax.rem(index + ahead, count)},
            device_id_type=MESH,
        )
        copy.start()
        return copy

    along = {}
    for ahead in range(1, ex_count):
        along[ahead] = push(
            own_ref, ex, "ex", ex, ex_count, ahead, send_ex.at[ahead], recv_ex.at[ahead]
        )
    for ahead in range(1, tp_count):
        started.append(push(
            own_ref, ex, "tp", tp, tp_count, ahead, send_tp.at[0, ahead], recv_tp.at[0, ahead]
        ))
    all_ref[ex, tp] = own_ref[...]
    for back in range(1, ex_count):
        along[back].wait_recv()
        block = lax.rem(ex + ex_count - back, ex_count)
        for ahead in range(1, tp_count):
            started.append(push(
                all_ref.at[block, tp], block, "tp", tp, tp_count, ahead,
                send_tp.at[back, ahead], recv_tp.at[back, ahead],
            ))
    for copy in started:
        copy.wait_recv()
    for copy in started:
        copy.wait_send()
    for copy in along.values():
        copy.wait_send()


def gather_all(own, small=None):
    ex_count, tp_count = lax.axis_size("ex"), lax.axis_size("tp")
    rows, lanes = own.shape
    if small is not None:
        dp_count = lax.axis_size("dp")
        gathered, smalls = pl.pallas_call(
            gather_small_kernel,
            out_shape=(
                jax.ShapeDtypeStruct((ex_count, tp_count, rows, lanes), own.dtype),
                jax.ShapeDtypeStruct((dp_count, ex_count) + small.shape, small.dtype),
            ),
            in_specs=[pl.BlockSpec(memory_space=pltpu.VMEM)] * 2,
            out_specs=[pl.BlockSpec(memory_space=pltpu.VMEM)] * 2,
            scratch_shapes=[
                pltpu.SemaphoreType.DMA((ex_count,)),
                pltpu.SemaphoreType.DMA((ex_count,)),
                pltpu.SemaphoreType.DMA((ex_count, tp_count)),
                pltpu.SemaphoreType.DMA((ex_count, tp_count)),
                pltpu.SemaphoreType.DMA((ex_count * dp_count,)),
                pltpu.SemaphoreType.DMA((ex_count * dp_count,)),
            ],
            compiler_params=pltpu.CompilerParams(collective_id=2, has_side_effects=True),
            name="gather_small",
        )(own, small)
        return gathered.reshape(ex_count, tp_count * rows, lanes), smalls
    gathered = pl.pallas_call(
        gather_kernel,
        out_shape=jax.ShapeDtypeStruct((ex_count, tp_count, rows, lanes), own.dtype),
        in_specs=[pl.BlockSpec(memory_space=pltpu.VMEM)],
        out_specs=pl.BlockSpec(memory_space=pltpu.VMEM),
        scratch_shapes=[
            pltpu.SemaphoreType.DMA((ex_count,)),
            pltpu.SemaphoreType.DMA((ex_count,)),
            pltpu.SemaphoreType.DMA((ex_count, tp_count)),
            pltpu.SemaphoreType.DMA((ex_count, tp_count)),
        ],
        compiler_params=pltpu.CompilerParams(collective_id=0, has_side_effects=True),
        name="gather_all",
    )(own)
    return gathered.reshape(ex_count, tp_count * rows, lanes)


def scatter_kernel(part_ref, base_ref, out_ref, from_tp, sums, from_ex,
                   send_tp, recv_tp, send_ex, recv_ex):
    ex_count, tp_count = part_ref.shape[:2]
    ex, tp = lax.axis_index("ex"), lax.axis_index("tp")
    greet()
    order = list(range(1, ex_count)) + [0]
    across = {}
    for back in order:
        block = lax.rem(ex + back, ex_count)
        for ahead in range(1, tp_count):
            peer = lax.rem(tp + ahead, tp_count)
            copy = pltpu.make_async_remote_copy(
                src_ref=part_ref.at[block, peer],
                dst_ref=from_tp.at[back, ahead - 1],
                send_sem=send_tp.at[back, ahead],
                recv_sem=recv_tp.at[back, ahead],
                device_id={"tp": peer},
                device_id_type=MESH,
            )
            copy.start()
            across[back, ahead] = copy
    along = {}
    for back in order:
        block = lax.rem(ex + back, ex_count)
        total = part_ref[block, tp].astype(jnp.float32)
        for ahead in range(1, tp_count):
            across[back, ahead].wait_recv()
            total = total + from_tp[back, ahead - 1].astype(jnp.float32)
        if back == 0:
            out_ref[...] = base_ref[...].astype(jnp.float32) + total
            continue
        sums[back] = total.astype(jnp.bfloat16)
        along[back] = pltpu.make_async_remote_copy(
            src_ref=sums.at[back],
            dst_ref=from_ex.at[back],
            send_sem=send_ex.at[back],
            recv_sem=recv_ex.at[back],
            device_id={"ex": block},
            device_id_type=MESH,
        )
        along[back].start()
    for copy in along.values():
        copy.wait_recv()
    total = out_ref[...]
    for back in along:
        total = total + from_ex[back].astype(jnp.float32)
    out_ref[...] = total
    for copy in across.values():
        copy.wait_send()
    for copy in along.values():
        copy.wait_send()


def scatter_sum(partial, base):
    ex_count, tp_count = lax.axis_size("ex"), lax.axis_size("tp")
    rows, lanes = base.shape
    total = pl.pallas_call(
        scatter_kernel,
        out_shape=jax.ShapeDtypeStruct((rows, lanes), jnp.float32),
        in_specs=[pl.BlockSpec(memory_space=pltpu.VMEM)] * 2,
        out_specs=pl.BlockSpec(memory_space=pltpu.VMEM),
        scratch_shapes=[
            pltpu.VMEM((ex_count, tp_count - 1, rows, lanes), jnp.bfloat16),
            pltpu.VMEM((ex_count, rows, lanes), jnp.bfloat16),
            pltpu.VMEM((ex_count, rows, lanes), jnp.bfloat16),
            pltpu.SemaphoreType.DMA((ex_count, tp_count)),
            pltpu.SemaphoreType.DMA((ex_count, tp_count)),
            pltpu.SemaphoreType.DMA((ex_count,)),
            pltpu.SemaphoreType.DMA((ex_count,)),
        ],
        compiler_params=pltpu.CompilerParams(collective_id=1, has_side_effects=True),
        name="scatter_sum",
    )(partial.reshape(ex_count, tp_count, rows, lanes), base)
    return total.astype(jnp.bfloat16)


def body(
    tokens,
    route_one,
    route_two,
    share_one,
    share_two,
    gain_one,
    gain_two,
    gate_up_one,
    down_one,
    gate_up_two,
    down_two,
):
    ex_count = lax.axis_size("ex")
    tp_count = lax.axis_size("tp")
    tokens_here, width = tokens.shape
    top_count = route_one.shape[1]
    local_count = gate_up_one.shape[0]
    experts = local_count * ex_count
    capacity = 2 * tokens_here * top_count // experts
    capacity = min(tokens_here, capacity)
    group = 2 if ex_count % 2 == 0 else 1
    col_share = width // tp_count
    columns = tokens.T
    own = lax.dynamic_slice_in_dim(columns, lax.axis_index("tp") * col_share, col_share, 0)

    target_one = placement(route_one, experts, capacity)
    target_two = placement(route_two, experts, capacity)
    small = jnp.concatenate(
        [target_one.T.astype(jnp.float32), target_two.T.astype(jnp.float32), share_one.T, share_two.T]
    )
    gathered, smalls = gather_all(own, small)
    smalls = smalls.reshape(-1, ex_count, 4, top_count, tokens_here)
    chosen = smalls[:, :, :2].astype(jnp.int32) // capacity
    mine = lax.axis_index("ex") * local_count + jnp.arange(local_count, dtype=jnp.int32)
    load = jnp.sum((chosen[..., None] == mine).astype(jnp.int32), axis=(0, 1, 3, 4))
    small = lax.dynamic_index_in_dim(smalls, lax.axis_index("dp"), 0, keepdims=False)
    choose_one, weight_one = choosers(small[:, 0], small[:, 2], local_count, capacity, group)
    choose_two, weight_two = choosers(small[:, 1], small[:, 3], local_count, capacity, group)

    first = experts_here(gathered, gain_one, choose_one, weight_one, gate_up_one, down_one, group)
    stream = scatter_sum(first, own)
    again = gather_all(stream)
    second = experts_here(again, gain_two, choose_two, weight_two, gate_up_two, down_two, group)
    mixed = scatter_sum(second, stream)
    return (mixed.T, load)


def solution(mesh):
    in_specs = (
        P(("ex", "dp"), None),
        P(("ex", "dp"), None),
        P(("ex", "dp"), None),
        P(("ex", "dp"), None),
        P(("ex", "dp"), None),
        P(),
        P(),
        P("ex", None, None, "tp"),
        P("ex", "tp", None),
        P("ex", None, None, "tp"),
        P("ex", "tp", None),
    )
    out_specs = (P(("ex", "dp"), "tp"), P(None, "ex"))
    return jax.shard_map(body, mesh=mesh, in_specs=in_specs, out_specs=out_specs, check_vma=False)
```

time: 735 us -> 247 us (0.34)
  blocking collectives: 291 us -> 0 us
  Pallas kernels: 0 us -> 223 us
  waiting for transfers between devices: 192 us -> 0 us
  local copies, waits for them, and re-layouts: 129 us -> 8.27 us
  matrix products: 76.3 us -> 0 us
  starting transfers between devices: 17.7 us -> 0 us
  between operations: 14.3 us -> 0.76 us
    all_to_all x2 -> x0, blocking collectives: 277 us -> none  [expert_layer(): lax.all_to_all(packed, 'ex', split_axis=0, concat_axis=0, tiled=True)]
    pallas_call x0 -> x6, Pallas kernels: none -> 223 us  [the longest x2 78.5 us: scatter_sum(): pl.pallas_call(scatter_kernel, out_shape=jax.ShapeDtypeStruct((rows, lane...]
    unnamed x4 -> x0, waiting for transfers between devices: 126 us -> none
    unnamed x20 -> x10, local copies, waits for them, and re-layouts: 92.6 us -> 1.69 us
    dot_general x6 -> x0, matrix products: 76.3 us -> none  [the longest x2 38.3 us: expert_layer(): jnp.einsum('secd,edf->secf', arrived, gate_up_flat, preferred_element_typ...]
    all_to_all x4 -> x0, waiting for transfers between devices: 65.3 us -> none  [the longest x2 65.3 us: expert_layer(): lax.all_to_all(expert_rows, 'ex', split_axis=0, concat_axis=0, tiled=True)]
    convert_element_type x5 -> x0, local copies, waits for them, and re-layouts: 18.1 us -> none  [the longest x2 17 us: pack_rows(): jnp.dot(chooser, normed, preferred_element_type=jnp.float32)]
    all_to_all x4 -> x0, starting transfers between devices: 17.6 us -> none  [the longest x2 9.82 us: expert_layer(): lax.all_to_all(expert_rows, 'ex', split_axis=0, concat_axis=0, tiled=True)]
  transfers between devices with their start and end apart: 6 -> 0, of which waited for: 4 -> 0; matrix products, arithmetic and copies ran while one was open for 2% -> 0% of each run, Pallas kernels for 0% -> 0%
where the time goes in v1:
time: 247 us; the launch traced here: 246 us
  Pallas kernels  223 us (90%)
  other arithmetic  14.7 us (6%)
  local copies, waits for them, and re-layouts  8.27 us (3%)
    pallas_call x2, Pallas kernels, scatter_sum(): pl.pallas_call(scatter_kernel, out_shape=jax.ShapeDtypeStruct((rows, lane...  78.5 us
    pallas_call x2, Pallas kernels, experts_here(): pl.pallas_call(functools.partial(expert_kernel, group), grid=(local_count...  64.5 us
    pallas_call x1, Pallas kernels, gather_all(): pl.pallas_call(gather_small_kernel, out_shape=(jax.ShapeDtypeStruct((ex_c...  42.4 us
    pallas_call x1, Pallas kernels, gather_all(): pl.pallas_call(gather_kernel, out_shape=jax.ShapeDtypeStruct((ex_count, t...  37.1 us

profile of v1, /device:TPU:0, one launch (start us, length us, event | category | flops | bytes accessed | tf_op | source)
XLA Modules:
  0.0 246.2 jit_solution(3640477923725824382)
XLA Ops:
  0.6 0.0 copy-start
  0.6 0.9 copy.41
  1.5 0.1 eq.103
  1.6 1.2 reduce-window.14
  2.8 0.2 slice_reduce_fusion.1
  3.0 0.1 eq.99
  3.2 0.1 fusion.6
  3.2 0.1 reduce_sum.50
  3.4 0.1 copy.44
  3.4 0.8 copy.45
  4.2 0.1 eq.111
  4.4 1.2 reduce-window.16
  5.5 0.2 slice_reduce_fusion
  5.8 0.1 eq.107
  5.9 0.1 fusion.4
  6.0 0.1 reduce_sum.52
  6.1 0.1 copy.48
  6.2 0.7 convert_bitcast_fusion.1
  6.9 1.3 pad_maximum_fusion.small_ref
  8.2 0.0 copy-done
  8.2 0.7 dynamic-slice_bitcast_fusion.own_ref.base_ref
  8.9 42.4 %gather_small.1 = (bf16[4,4,720,128]{3,2,1,0:T(8,128)(2,1)}, f32[2,4,16,128]{3,2,1,0:T(8,128)}) custom-call(bf16[720,128]{1,0:T(8,128)(2,1)} %dynamic-slice_bitcast_fusion.own_ref.base_ref, f32[16,128]{1,0:T(8,128)} %pad_maximum_fusion.small_ref), custom_call_target="tpu_custom_call" | custom-call | tf_op jit(solution)/shard_map/gather_small/pallas_call | solution.py:237
  51.3 0.8 dynamic-slice_bitcast_fusion.1
  52.1 0.1 fusion.19
  52.2 1.3 select_reduce_fusion.1
  53.5 0.7 fusion.1
  54.2 0.8 convert_element_type.57.choose_ref
  55.1 2.3 broadcast_in_dim.46.gain_ref
  57.4 32.1 %experts_here.2 = bf16[4,2880,128]{2,1,0:T(8,128)(2,1)} custom-call(bf16[4,2880,128]{2,1,0:T(8,128)(2,1)} %bitcast.135, f32[2880,1]{1,0:T(8,128)} %broadcast_in_dim.46.gain_ref, bf16[2,256,512]{2,1,0:T(8,128)(2,1)} %convert_element_type.57.choose_ref, f32[4,1,256]{2,1,0:T(1,128)} %bitcast.142, bf16[4,1440,2880]{2,1,0:T(8,128)(2,1)} %bitcast.130, ...), custom_call_target="tpu_custom_call" | custom-call | flops 12740198400 | bytes 49766400 | tf_op jit(solution)/shard_map/experts_here/pallas_call | solution.py:96
  89.5 0.0 copy-start.3
  89.5 40.3 %scatter_sum.2 = f32[720,128]{1,0:T(8,128)} custom-call(bf16[4,4,720,128]{3,2,1,0:T(8,128)(2,1)} %bitcast.133, bf16[720,128]{1,0:T(8,128)(2,1)} %dynamic-slice_bitcast_fusion.own_ref.base_ref), custom_call_target="tpu_custom_call" | custom-call | tf_op jit(solution)/shard_map/scatter_sum/pallas_call | solution.py:330
  129.8 1.7 convert_element_type.58.own_ref.base_ref
  131.5 37.1 %gather_all.1 = bf16[4,4,720,128]{3,2,1,0:T(8,128)(2,1)} custom-call(bf16[720,128]{1,0:T(8,128)(2,1)} %convert_element_type.58.own_ref.base_ref), custom_call_target="tpu_custom_call" | custom-call | tf_op jit(solution)/shard_map/gather_all/pallas_call | solution.py:257
  168.6 1.3 select_reduce_fusion
  169.9 0.7 fusion
  170.7 0.8 convert_element_type.60.choose_ref
  171.5 0.0 copy-done.3
  171.5 1.6 broadcast_in_dim.47.gain_ref
  173.1 0.0 copy-start.2
  173.1 0.0 copy-start.1
  173.1 32.3 %experts_here.3 = bf16[4,2880,128]{2,1,0:T(8,128)(2,1)} custom-call(bf16[4,2880,128]{2,1,0:T(8,128)(2,1)} %bitcast.132, f32[2880,1]{1,0:T(8,128)} %broadcast_in_dim.47.gain_ref, bf16[2,256,512]{2,1,0:T(8,128)(2,1)} %convert_element_type.60.choose_ref, f32[4,1,256]{2,1,0:T(1,128)} %bitcast.143, bf16[4,1440,2880]{2,1,0:T(8,128)(2,1)} %bitcast.131, ...), custom_call_target="tpu_custom_call" | custom-call | flops 12740198400 | bytes 49766400 | tf_op jit(solution)/shard_map/experts_here/pallas_call | solution.py:96
  205.5 38.2 %scatter_sum.3 = f32[720,128]{1,0:T(8,128)} custom-call(bf16[4,4,720,128]{3,2,1,0:T(8,128)(2,1)} %bitcast.134, bf16[720,128]{1,0:T(8,128)(2,1)} %convert_element_type.58.own_ref.base_ref), custom_call_target="tpu_custom_call" | custom-call | tf_op jit(solution)/shard_map/scatter_sum/pallas_call | solution.py:330
  243.7 1.7 convert_bitcast_fusion
  245.4 0.0 copy-done.2
  245.5 0.8 convert_reduce_fusion
  246.2 0.0 copy-done.1
  (11 shorter events, 0.2 us)
Async XLA Ops:
  0.6 7.6 %copy-start = (bf16[128,2880]{0,1:T(8,128)(2,1)S(1)}, bf16[128,2880]{0,1:T(8,128)(2,1)}, u32[]{:S(2)}) copy-start(bf16[128,2880]{0,1:T(8,128)(2,1)} %param.11) | copy-start | bytes 2211844
  89.5 82.1 %copy-start.3 = (f32[2880]{0:T(1024)S(1)}, f32[2880]{0:T(1024)}, u32[]{:S(2)}) copy-start(f32[2880]{0:T(1024)} %param.17) | copy-start | bytes 34564
  173.1 72.2 %copy-start.2 = (f32[2,4,16,128]{3,2,1,0:T(8,128)S(1)}, f32[2,4,16,128]{3,2,1,0:T(8,128)}, u32[]{:S(2)}) copy-start(f32[2,4,16,128]{3,2,1,0:T(8,128)} %get-tuple-element.5) | copy-start | bytes 196612
  173.1 73.1 %copy-start.1 = (bf16[128,2880]{0,1:T(8,128)(2,1)S(1)}, bf16[128,2880]{0,1:T(8,128)(2,1)}, u32[]{:S(2)}) copy-start(bf16[128,2880]{0,1:T(8,128)(2,1)} %param.11) | copy-start | bytes 2211844
